TPU v7x, 32 devices: a whole 2x2x4 slice. The times are simulated.
32 devices in a mesh: seq: 8 (over z, y), chan: 4 (over x, core).
Axes of the slice: x: 2, y: 2, z: 4, core: 2. Of those that a mesh axis runs over, the one named last changes fastest.
Arguments:
- hidden_in: bfloat16 [1024, 2048], P('seq', 'chan'), may hold values from -6 to 6
- norm_gain: float32 [2048], replicated, may hold values from 0.5 to 1.5
- in_weight: bfloat16 [2048, 2, 4096], P('seq', None, 'chan'), may hold values from -0.125 to 0.125
- conv_weight: float32 [2, 4, 4096], P(None, None, 'chan'), may hold values from -3 to 3
- conv_bias: float32 [2, 4096], P(None, 'chan'), may hold values from -0.5 to 0.5
- proj_weight: bfloat16 [2, 4096, 160], P(None, 'chan'), may hold values from -0.1875 to 0.1875
- step_weight: bfloat16 [2, 128, 4096], P(None, None, 'chan'), may hold values from -0.5 to 0.5
- decay_rate: float32 [2, 4096], P(None, 'chan'), may hold values from 0.00024414062 to 0.25
- skip_gain: float32 [2, 4096], P(None, 'chan'), may hold values from 0.5 to 1.5
- out_weight: bfloat16 [4096, 2048], P('chan', 'seq'), may hold values from -0.09375 to 0.09375
Outputs:
- mixed: bfloat16 [1024, 2048], P('seq', 'chan')
All inputs are finite; a program needn't handle non-finite values.
Results may differ from a plain program's by a relative error of at most 0.0095.
Values may be sent and summed in bfloat16 or wider, within the bound.
No kernel may reach another device: no remote copies, remote signals or barrier semaphores. Data moves between devices by JAX's collectives and lax.ppermute only.
A program may use at most 128 MiB of HBM per device.

v0:
```python
import jax
import jax.numpy as jnp
from jax import lax
from jax.sharding import PartitionSpec as P

STATE = 16
WIDTH = 4


def with_halo(block, sides, width):
    for axis, dim in sides:
        count = lax.axis_size(axis)
        forward = [(i, i + 1) for i in range(count - 1)]
        backward = [(target, source) for source, target in forward]
        low = lax.ppermute(
            lax.slice_in_dim(block, block.shape[dim] - width, None, axis=dim), axis, forward
        )
        high = lax.ppermute(lax.slice_in_dim(block, 0, width, axis=dim), axis, backward)
        block = jnp.concatenate([low, block, high], axis=dim)
    return block


def entering(array, axis, combine, identity, reverse):
    devices, here = (lax.axis_size(axis), lax.axis_index(axis))
    everything = jax.tree.map(lambda part: lax.all_gather(part, axis), array)
    start = jax.tree.map(
        lambda part, zero: jnp.broadcast_to(jnp.asarray(zero, part.dtype), part.shape),
        array,
        identity,
    )

    def hop(k, before):
        at = devices - 1 - k if reverse else k
        reached = at > here if reverse else at < here
        new = combine(before, jax.tree.map(lambda part: part[at], everything))
        return jax.tree.map(lambda a, b: jnp.where(reached, a, b), new, before)

    return lax.fori_loop(0, devices, hop, start)


def conv_taps(padded, conv_weight, conv_bias, length):
    reach = conv_weight.shape[1] - 1
    forward = jnp.zeros((length, padded.shape[1]), jnp.float32) + conv_bias[0][None, :]
    backward = jnp.zeros((length, padded.shape[1]), jnp.float32) + conv_bias[1][None, :]
    for offset in range(reach + 1):
        forward = forward + conv_weight[0, offset][None, :] * padded[offset : offset + length]
        begin = 2 * reach - offset
        backward = backward + conv_weight[1, offset][None, :] * padded[begin : begin + length]
    return jax.nn.silu(jnp.stack([forward, backward])).astype(jnp.bfloat16)


def sweep(drive_values, key_rows, query_rows, epsilon, initial, reverse, keeping):
    product = jnp.ones(initial.shape, jnp.float32)

    def advance(carry, current):
        product, state = carry
        drive_row, key_row, query_row, eps_row = current
        decay = 1.0 - eps_row[None, :] * (key_row * key_row)[:, None]
        state = decay * state + key_row[:, None] * (eps_row * drive_row)[None, :]
        product = decay * product
        if keeping == "reads":
            output = jnp.sum(query_row[:, None] * state, axis=0)
        else:
            output = None
        return ((product, state), output)

    (product, state), outputs = lax.scan(
        advance,
        (product, initial),
        (drive_values, key_rows, query_rows, epsilon),
        reverse=reverse,
        unroll=16,
    )
    return (product, state, outputs)


def combine(earlier, latter):
    return (latter[0] * earlier[0], latter[0] * earlier[1] + latter[1])


def per_device(
    hidden_in,
    norm_gain,
    in_weight,
    conv_weight,
    conv_bias,
    proj_weight,
    step_weight,
    decay_rate,
    skip_gain,
    out_weight,
):
    gathered = lax.all_gather(hidden_in, "chan", axis=1, tiled=True).astype(jnp.float32)
    normed = (
        gathered
        * lax.rsqrt(jnp.mean(gathered * gathered, axis=1, keepdims=True) + 1e-05)
        * norm_gain[None, :]
    ).astype(jnp.bfloat16)
    row_count = normed.shape[0]
    channels = in_weight.shape[2]
    piece = lax.all_gather(in_weight, "seq", axis=0, tiled=True)
    projected = jnp.dot(
        normed, piece.reshape(piece.shape[0], 2 * channels), preferred_element_type=jnp.float32
    )
    projected = projected.astype(jnp.bfloat16).reshape(row_count, 2, channels)
    branch = projected[:, 0, :]
    gate_half = projected[:, 1, :].astype(jnp.float32)
    padded = with_halo(branch, (("seq", 0),), WIDTH - 1).astype(jnp.float32)
    driven = conv_taps(padded, conv_weight, conv_bias, row_count)
    partial_value = jnp.einsum(
        "dte,def->tdf", driven, proj_weight, preferred_element_type=jnp.float32
    )
    features = lax.psum(partial_value, "chan")
    key_rows = features[:, :, :STATE]
    query_rows = features[:, :, STATE : 2 * STATE]
    low_rank = features[:, :, 2 * STATE :].astype(jnp.bfloat16)
    step_size = jnp.einsum(
        "tdr,dre->tde", low_rank, step_weight, preferred_element_type=jnp.float32
    )
    beta_rows = 2.0 * decay_rate[None, :, :] * jax.nn.sigmoid(step_size)
    epsilon = beta_rows / (1.0 + beta_rows * jnp.sum(key_rows * key_rows, axis=2, keepdims=True))
    drive_values = driven.astype(jnp.float32)
    zero_state = jnp.zeros((STATE, channels), jnp.float32)
    keeping = "summary"
    passes = [
        sweep(
            drive_values[direction],
            key_rows[:, direction],
            query_rows[:, direction],
            epsilon[:, direction],
            zero_state,
            direction == 1,
            keeping,
        )
        for direction in range(2)
    ]
    identity = (jnp.ones((STATE, channels), jnp.float32), zero_state)
    incoming_forward = entering((passes[0][0], passes[0][1]), "seq", combine, identity, False)[1]
    incoming_reverse = entering((passes[1][0], passes[1][1]), "seq", combine, identity, True)[1]
    incoming = [incoming_forward, incoming_reverse]
    total = jnp.zeros((row_count, channels), jnp.float32)
    for direction in range(2):
        reads = sweep(
            drive_values[direction],
            key_rows[:, direction],
            query_rows[:, direction],
            epsilon[:, direction],
            incoming[direction],
            direction == 1,
            "reads",
        )[2]
        total = total + reads + skip_gain[direction][None, :] * drive_values[direction]
    combined = (total * jax.nn.silu(gate_half)).astype(jnp.bfloat16)
    partial_out = jnp.dot(
        combined,
        lax.all_gather(out_weight, "seq", axis=1, tiled=True),
        preferred_element_type=jnp.float32,
    )
    summed = lax.psum(partial_out, "chan")
    share_width = summed.shape[1] // lax.axis_size("chan")
    share = lax.dynamic_slice_in_dim(summed, lax.axis_index("chan") * share_width, share_width, 1)
    return share.astype(jnp.bfloat16)


def solution(mesh):
    in_specs = (
        P("seq", "chan"),
        P(),
        P("seq", None, "chan"),
        P(None, None, "chan"),
        P(None, "chan"),
        P(None, "chan", None),
        P(None, None, "chan"),
        P(None, "chan"),
        P(None, "chan"),
        P("chan", "seq"),
    )
    out_specs = P("seq", "chan")
    return jax.shard_map(
        per_device, mesh=mesh, in_specs=in_specs, out_specs=out_specs, check_vma=False
    )
```

profile of v0, /device:TPU:0, one launch (start us, length us, event | category | flops | bytes accessed | tf_op | source)
XLA Modules:
  0.0 489.7 jit_solution(10717089666315897083)
XLA Ops:
  7.3 8.9 %all_gather.33 = bf16[128,2048]{1,0:T(8,128)(2,1)S(1)} all-gather(bf16[128,512]{1,0:T(8,128)(2,1)} %param.22), channel_id=1, replica_groups=mesh['seq'=8,'chan'=4] {'chan'}, dimensions={1}, use_global_device_ids=true | all-gather | bytes 655360 | tf_op jit(solution)/shard_map/all_gather | solution.py:93
  18.1 118.6 %all-gather.7.cloned.1.call-done = bf16[2048,2,1024]{2,1,0:T(2,128)(2,1)} async-done(((bf16[256,2,1024]{2,1,0:T(2,128)(2,1)}), bf16[2048,2,1024]{2,1,0:T(2,128)(2,1)}) %all-gather.7.cloned.1.call-update) | async-done | bytes 8388624 | tf_op jit(solution)/shard_map/all_gather | solution.py:101
  136.7 10.1 %copy.42 = bf16[256,8,2,1024]{3,1,2,0:T(8,128)(2,1)} copy(bf16[256,8,2,1024]{3,2,1,0:T(2,128)(2,1)} %bitcast.855) | data formatting | bytes 16777216
  146.8 4.7 convolution_convert_fusion
  153.3 4.5 collective-permute-start
  163.2 30.7 %all-reduce.3.cloned.1.call-done = f32[128,2,160]{0,2,1:T(8,128)} async-done(((f32[128,2,160]{0,2,1:T(8,128)}), f32[128,2,160]{0,2,1:T(8,128)}) %all-reduce.3.cloned.1.call-update) | async-done | bytes 163856 | tf_op jit(solution)/shard_map/psum | solution.py:113
  199.1 22.7 %while.92 = (s32[]{:T(128)}, f32[16,1024]{1,0:T(8,128)S(1)}, f32[16,1024]{1,0:T(8,128)S(1)}, f32[8,16,1024]{2,1,0:T(8,128)}, f32[8,16,16]{2,1,0:T(8,128)S(1)}, /...) while((s32[]{:T(128)}, f32[16,1024]{1,0:T(8,128)S(1)}, ...), condition=%wide.region_26.27_spmd.clone, body=%wide.region_25.26_spmd.clone.sunk | while | flops 2146579 | bytes 924200 | solution.py:67
  199.1 2.0 constant_dynamic-slice_fusion.231
  202.1 2.0 constant_dynamic-slice_fusion.231
  207.8 1.8 constant_dynamic-slice_fusion.231
  210.6 2.0 constant_dynamic-slice_fusion.231
  213.5 2.0 constant_dynamic-slice_fusion.231
  219.2 1.8 constant_dynamic-slice_fusion.231
  221.8 9.5 %while.90 = (s32[]{:T(128)}, f32[16,1024]{1,0:T(8,128)S(1)}, f32[16,1024]{1,0:T(8,128)S(1)}, f32[8,16,1024]{2,1,0:T(8,128)S(1)}, f32[8,16,16]{2,1,0:T(8,128)S(1)...) while((s32[]{:T(128)}, f32[16,1024]{1,0:T(8,128)S(1)}, ...), condition=%wide.region_4.5_spmd.clone, body=%wide.region_3.4_spmd.clone.sunk | while | flops 2146578 | bytes 924180 | solution.py:67
  231.3 37.0 %all-gather.1 = f32[128,1024]{1,0:T(8,128)} all-gather(f32[16,1024]{1,0:T(8,128)S(1)} %get-tuple-element.566), channel_id=3, replica_groups=mesh['seq'=8,'chan'=4] {'seq'}, dimensions={0}, use_global_device_ids=true | all-gather | bytes 589824 | tf_op jit(solution)/shard_map/all_gather | solution.py:25
  268.3 34.7 %all-gather.3 = f32[128,1024]{1,0:T(8,128)} all-gather(f32[16,1024]{1,0:T(8,128)S(1)} %get-tuple-element.570), channel_id=5, replica_groups=mesh['seq'=8,'chan'=4] {'seq'}, dimensions={0}, use_global_device_ids=true | all-gather | bytes 589824 | tf_op jit(solution)/shard_map/all_gather | solution.py:25
  303.0 33.4 %all-gather = f32[128,1024]{1,0:T(8,128)} all-gather(f32[16,1024]{1,0:T(8,128)S(1)} %get-tuple-element.565), channel_id=2, replica_groups=mesh['seq'=8,'chan'=4] {'seq'}, dimensions={0}, use_global_device_ids=true | all-gather | bytes 589824 | tf_op jit(solution)/shard_map/all_gather | solution.py:25
  336.4 7.5 %while.91 = (s32[]{:T(128)}, f32[16,1024]{1,0:T(8,128)S(1)}, s32[]{:T(128)}, f32[8,16,1024]{2,1,0:T(8,128)}, f32[8,16,1024]{2,1,0:T(8,128)}, /*index=5*/s32[]{:T(128)}, s32[]{:T(128)}) while((s32[]{:T(128)}, f32[16,1024]{1,0:T(8,128)S(1)}, s32[]{:T(128)}, f32[8,16,1024]{2,1,0:T(8,128)}, f32[8,16,1024]{2,1,0:T(8,128)}, ...), condition=%wide.region_6.7_spmd.clone, body=%wide.region_5.6_spmd.clone.sunk | while | flops 65540 | bytes 262253 | solution.py:38
  343.9 33.6 %all-gather.2 = f32[128,1024]{1,0:T(8,128)} all-gather(f32[16,1024]{1,0:T(8,128)S(1)} %get-tuple-element.569), channel_id=4, replica_groups=mesh['seq'=8,'chan'=4] {'seq'}, dimensions={0}, use_global_device_ids=true | all-gather | bytes 589824 | tf_op jit(solution)/shard_map/all_gather | solution.py:25
  377.5 7.5 %while.93 = (s32[]{:T(128)}, f32[16,1024]{1,0:T(8,128)S(1)}, s32[]{:T(128)}, f32[8,16,1024]{2,1,0:T(8,128)}, f32[8,16,1024]{2,1,0:T(8,128)}, /*index=5*/s32[]{:T(128)}, s32[]{:T(128)}, s32[]{:T(128)}, s32[]{:T(128)}) while((s32[]{:T(128)}, f32[16,1024]{1,0:T(8,128)S(1)}, s32[]{:T(128)}, f32[8,16,1024]{2,1,0:T(8,128)}, ...), condition=%wide.region_28.29_spmd.clone, body=%wide.region_27.28_spmd.clone.sunk | while | flops 65544 | bytes 262315 | solution.py:38
  385.9 33.0 %while.89 = (s32[]{:T(128)}, f32[16,1024]{1,0:T(8,128)S(1)}, f32[8,16,1024]{2,1,0:T(8,128)}, f32[8,16,1024]{2,1,0:T(8,128)}, f32[8,16,16]{2,1,0:T(8,128)S(1)}, /...) while((s32[]{:T(128)}, f32[16,1024]{1,0:T(8,128)S(1)}, ...), condition=%wide.region_46.47_spmd, body=%wide.region_29.46_spmd.sunk | while | flops 2408722 | bytes 2033121 | solution.py:67
  386.1 2.0 constant_dynamic-slice_fusion.229
  390.3 2.0 constant_dynamic-slice_fusion.229
  394.6 1.8 constant_dynamic-slice_fusion.229
  398.6 1.8 constant_dynamic-slice_fusion.229
  402.6 2.0 constant_dynamic-slice_fusion.229
  406.8 2.0 constant_dynamic-slice_fusion.229
  411.0 1.8 constant_dynamic-slice_fusion.229
  415.0 1.8 constant_dynamic-slice_fusion.229
  418.9 32.4 %while.88 = (s32[]{:T(128)}, f32[16,1024]{1,0:T(8,128)S(1)}, f32[8,16,1024]{2,1,0:T(8,128)S(1)}, f32[8,16,1024]{2,1,0:T(8,128)S(1)}, f32[8,16,16]{2,1,0:T(8,128)...) while((s32[]{:T(128)}, f32[16,1024]{1,0:T(8,128)S(1)}, ...), condition=%wide.region_24.25_spmd, body=%wide.region_7.24_spmd.sunk | while | flops 2490641 | bytes 2106965 | solution.py:67
  452.8 2.9 fusion.342
  455.7 26.7 %all-reduce.4 = bf16[128,2048]{1,0:T(8,128)(2,1)S(1)} all-reduce(f32[128,2048]{1,0:T(8,128)S(1)} %fusion.342), channel_id=1, replica_groups=mesh['seq'=8,'chan'=4] {'chan'}, use_global_device_ids=true, to_apply=%region_47.48 | all-reduce | flops 262144 | bytes 1572864 | tf_op jit(solution)/shard_map/psum | solution.py:159
  (853 shorter events, 97.4 us)
Async XLA Ops:
  6.5 153.8 %copy-start = (bf16[2,1024,160]{1,2,0:T(8,128)(2,1)S(1)}, bf16[2,1024,160]{1,2,0:T(8,128)(2,1)}, u32[]{:S(2)}) copy-start(bf16[2,1024,160]{1,2,0:T(8,128)(2,1)} %param.27) | copy-start | bytes 1966084
  6.5 130.2 %all-gather.7.cloned.1.call-start = ((), (), s32[]{:S(2)}) async-start(), calls=%async_computation | async-start | bytes 9437184 | tf_op jit(solution)/shard_map/all_gather | solution.py:101
  7.3 186.6 %all-reduce.3.cloned.1.call-start = ((), (), s32[]{:S(2)}) async-start(), calls=%async_computation.1 | async-start | bytes 327680 | tf_op jit(solution)/shard_map/psum | solution.py:113
  136.7 10.1 %copy-start.4 = (f32[2048]{0:T(1024)S(1)}, f32[2048]{0:T(1024)}, u32[]{:S(2)}) copy-start(f32[2048]{0:T(1024)} %param.23) | copy-start | bytes 24580
  151.5 10.6 %copy-start.5 = (f32[2,1024]{1,0:T(2,128)S(1)}, f32[2,1024]{1,0:T(2,128)}, u32[]{:S(2)}) copy-start(f32[2,1024]{1,0:T(2,128)} %param.29) | copy-start | bytes 24580
  151.5 10.7 %copy-start.6 = (f32[2,1024]{1,0:T(2,128)S(1)}, f32[2,1024]{1,0:T(2,128)}, u32[]{:S(2)}) copy-start(f32[2,1024]{1,0:T(2,128)} %param.30) | copy-start | bytes 24580
  152.0 7.5 %collective-permute-start.1 = (bf16[3,1024]{1,0:T(4,128)(2,1)S(1)}, bf16[3,1024]{1,0:T(4,128)(2,1)S(1)}, u32[]{:S(2)}, u32[]{:S(2)}) collective-permute-start(bf16[3,1024]{1,0:T(4,128)(2,1)S(1)} %bitcast.1151), channel_id=1, source_target_pairs={{4,0},{8,4},{12,8},{16,12},{20,16},{24,20},{28,24},{5,1},{9,5},{13... | collective-permute-start | bytes 18440 | tf_op jit(solution)/shard_map/ppermute | solution.py:18
  153.3 6.2 %collective-permute-start = (bf16[3,1024]{1,0:T(4,128)(2,1)S(1)}, bf16[3,1024]{1,0:T(4,128)(2,1)S(1)}, u32[]{:S(2)}, u32[]{:S(2)}) collective-permute-start(bf16[3,1024]{1,0:T(4,128)(2,1)S(1)} %bitcast.1150), channel_id=1, source_target_pairs={{0,4},{4,8},{8,12},{12,16},{16,20},{20,24},{24,28},{1,5},{5,9},{9,... | collective-permute-start | bytes 18440 | tf_op jit(solution)/shard_map/ppermute | solution.py:15
  161.4 291.4 %all-gather.9.cloned.1.call-start = ((), (), s32[]{:S(2)}) async-start(), calls=%async_computation.2 | async-start | bytes 4718592 | tf_op jit(solution)/shard_map/all_gather | solution.py:156
  163.2 35.9 %copy-start.1 = (f32[16,1024]{1,0:T(8,128)S(1)}, f32[16,1024]{1,0:T(8,128)}, u32[]{:S(2)}) copy-start(f32[16,1024]{1,0:T(8,128)} %custom-call.4) | copy-start | bytes 196612
  163.2 35.9 %copy-start.2 = (f32[16,1024]{1,0:T(8,128)S(1)}, f32[16,1024]{1,0:T(8,128)}, u32[]{:S(2)}) copy-start(f32[16,1024]{1,0:T(8,128)} %custom-call.3) | copy-start | bytes 196612
  231.3 154.6 %copy-start.3 = (f32[8,16,16]{2,1,0:T(8,128)}, f32[8,16,16]{2,1,0:T(8,128)S(1)}, u32[]{:S(2)}) copy-start(f32[8,16,16]{2,1,0:T(8,128)S(1)} %get-tuple-element.2563) | copy-start | bytes 24580
Sparse Core Ops, SparseCore 0:
  9.5 127.1 all-gather.6
  161.5 32.3 all-reduce.2
  195.9 86.4 all-gather.8
where the time goes:
time: 494 us; the launch traced here: 490 us
  blocking collectives  174 us (35%)
  waiting for transfers between devices  151 us (31%)
  local copies, waits for them, and re-layouts  69.2 us (14%)
  other arithmetic  59.8 us (12%)
  between operations  13.4 us (3%)
  matrix products  10.3 us (2%)
  loops' own time  6.06 us (1%)
  starting transfers between devices  5.92 us (1%)
    all_gather x4, blocking collectives, entering(): everything = jax.tree.map(lambda part: lax.all_gather(part, axis), array)  139 us
    all_gather x1, waiting for transfers between devices, per_device(): piece = lax.all_gather(in_weight, 'seq', axis=0, tiled=True)  119 us
    slice x32, local copies, waits for them, and re-layouts, sweep(): lax.scan(advance, (product, initial), (drive_values, key_rows, query_rows...  34.3 us
    psum x1, waiting for transfers between devices, per_device(): features = lax.psum(partial_value, 'chan')  30.7 us
    psum x1, blocking collectives, per_device(): summed = lax.psum(partial_out, 'chan')  26.7 us
    reduce_sum x136, other arithmetic, advance(): output = jnp.sum(query_row[:, None] * state, axis=0)  17.7 us
    select_n x16, other arithmetic, hop(): return jax.tree.map(lambda a, b: jnp.where(reached, a, b), new, before)  14.6 us
    mul x32, other arithmetic, advance(): decay = 1.0 - eps_row[None, :] * (key_row * key_row)[:, None]  12.7 us
  transfers between devices with their start and end apart: 5, of which 2 were waited for; matrix products, arithmetic and copies ran while one was open for 24% of the time, Pallas kernels for 0%

commit v1 on v0

--- a/solution.py
+++ b/solution.py
@@ -110,7 +110,7 @@
     partial_value = jnp.einsum(
         "dte,def->tdf", driven, proj_weight, preferred_element_type=jnp.float32
     )
-    features = lax.psum(partial_value, "chan")
+    features = lax.all_gather(partial_value, "chan").sum(axis=0)
     key_rows = features[:, :, :STATE]
     query_rows = features[:, :, STATE : 2 * STATE]
     low_rank = features[:, :, 2 * STATE :].astype(jnp.bfloat16)

time: 494 us -> 507 us (1.026)
  other arithmetic: 59.8 us -> 97.6 us
  waiting for transfers between devices: 151 us -> 118 us
    psum x1 -> x0, waiting for transfers between devices: 30.7 us -> none  [per_device(): features = lax.psum(partial_value, 'chan')]
    mul x32, other arithmetic: 12.7 us -> 27.3 us  [advance(): decay = 1.0 - eps_row[None, :] * (key_row * key_row)[:, None]]
    add x16, other arithmetic: 5.87 us -> 16.8 us  [advance(): state = decay * state + key_row[:, None] * (eps_row * drive_row)[None, :]]
    mul x16, other arithmetic: 3.1 us -> 13.8 us  [advance(): product = decay * product]
    mul x16, local copies, waits for them, and re-layouts: 8.66 us -> 16.8 us  [advance(): output = jnp.sum(query_row[:, None] * state, axis=0)]
    all_gather x0 -> x1, blocking collectives: none -> 8.1 us  [per_device(): features = lax.all_gather(partial_value, 'chan').sum(axis=0)]
  transfers between devices with their start and end apart: 5 -> 4, of which waited for: 2 -> 1; matrix products, arithmetic and copies ran while one was open for 24% -> 35% of each run, Pallas kernels for 0% -> 0%
where the time goes in v1:
time: 507 us; the launch traced here: 501 us
  blocking collectives  177 us (35%)
  waiting for transfers between devices  118 us (23%)
  other arithmetic  97.6 us (19%)
  local copies, waits for them, and re-layouts  73.7 us (15%)
  between operations  13.7 us (3%)
  matrix products  9.63 us (2%)
  loops' own time  5.97 us (1%)
  starting transfers between devices  5.88 us (1%)
    all_gather x4, blocking collectives, entering(): everything = jax.tree.map(lambda part: lax.all_gather(part, axis), array)  135 us
    all_gather x1, waiting for transfers between devices, per_device(): piece = lax.all_gather(in_weight, 'seq', axis=0, tiled=True)  116 us
    slice x32, local copies, waits for them, and re-layouts, sweep(): lax.scan(advance, (product, initial), (drive_values, key_rows, query_rows...  33.4 us
    mul x32, other arithmetic, advance(): decay = 1.0 - eps_row[None, :] * (key_row * key_row)[:, None]  27.3 us
    psum x1, blocking collectives, per_device(): summed = lax.psum(partial_out, 'chan')  25.5 us
    reduce_sum x136, other arithmetic, advance(): output = jnp.sum(query_row[:, None] * state, axis=0)  17.7 us
    mul x16, local copies, waits for them, and re-layouts, advance(): output = jnp.sum(query_row[:, None] * state, axis=0)  16.8 us
    add x16, other arithmetic, advance(): state = decay * state + key_row[:, None] * (eps_row * drive_row)[None, :]  16.8 us
  transfers between devices with their start and end apart: 4, of which 1 were waited for; matrix products, arithmetic and copies ran while one was open for 35% of the time, Pallas kernels for 0%

profile of v1, /device:TPU:0, one launch (start us, length us, event | category | flops | bytes accessed | tf_op | source)
XLA Modules:
  0.0 501.2 jit_solution(18373733635236604662)
XLA Ops:
  11.3 8.9 %all_gather.39 = bf16[128,2048]{1,0:T(8,128)(2,1)S(1)} all-gather(bf16[128,512]{1,0:T(8,128)(2,1)} %param.22), channel_id=1, replica_groups=mesh['seq'=8,'chan'=4] {'chan'}, dimensions={1}, use_global_device_ids=true | all-gather | bytes 655360 | tf_op jit(solution)/shard_map/all_gather | solution.py:93
  20.3 116.3 %all-gather.8.cloned.1.call-done = bf16[2048,2,1024]{2,1,0:T(2,128)(2,1)} async-done(((bf16[256,2,1024]{2,1,0:T(2,128)(2,1)}), bf16[2048,2,1024]{2,1,0:T(2,128)(2,1)}) %all-gather.8.cloned.1.call-update) | async-done | bytes 8388624 | tf_op jit(solution)/shard_map/all_gather | solution.py:101
  136.7 10.1 %copy.46 = bf16[256,8,2,1024]{3,1,2,0:T(8,128)(2,1)} copy(bf16[256,8,2,1024]{3,2,1,0:T(2,128)(2,1)} %bitcast.857) | data formatting | bytes 16777216
  146.8 4.7 convolution_convert_fusion
  153.3 4.5 collective-permute-start
  160.7 8.1 %all-gather = f32[512,2,160]{0,2,1:T(8,128)S(1)} all-gather(f32[128,2,160]{0,2,1:T(8,128)S(1)} %convolution_bitcast_fusion), channel_id=2, replica_groups=mesh['seq'=8,'chan'=4] {'chan'}, dimensions={0}, use_global_device_ids=true | all-gather | bytes 819200 | tf_op jit(solution)/shard_map/all_gather | solution.py:113
  177.1 50.6 %while.92 = (s32[]{:T(128)}, f32[16,1024]{1,0:T(8,128)}, f32[16,1024]{1,0:T(8,128)}, f32[8,16,1024]{2,1,0:T(8,128)}, f32[8,16,16]{2,1,0:T(8,128)}, /*index=5*/f3...) while((s32[]{:T(128)}, f32[16,1024]{1,0:T(8,128)}, ...), condition=%wide.region_26.27_spmd.clone, body=%wide.region_25.26_spmd.clone.sunk | while | flops 2146579 | bytes 924200 | solution.py:67
  178.3 2.0 constant_dynamic-slice_fusion.231
  185.2 1.8 multiply_add_fusion.53
  189.7 2.0 constant_dynamic-slice_fusion.231
  191.9 1.8 multiply_add_fusion.53
  198.3 1.8 multiply_add_fusion.53
  204.7 1.8 multiply_add_fusion.53
  209.2 2.0 constant_dynamic-slice_fusion.231
  211.4 1.8 multiply_add_fusion.53
  217.8 1.8 multiply_add_fusion.53
  224.3 1.8 multiply_add_fusion.53
  227.8 9.6 %while.90 = (s32[]{:T(128)}, f32[16,1024]{1,0:T(8,128)S(1)}, f32[16,1024]{1,0:T(8,128)S(1)}, f32[8,16,1024]{2,1,0:T(8,128)S(1)}, f32[8,16,16]{2,1,0:T(8,128)S(1)...) while((s32[]{:T(128)}, f32[16,1024]{1,0:T(8,128)S(1)}, ...), condition=%wide.region_4.5_spmd.clone, body=%wide.region_3.4_spmd.clone.sunk | while | flops 2146578 | bytes 924180 | solution.py:67
  237.3 34.4 %all-gather.2 = f32[128,1024]{1,0:T(8,128)} all-gather(f32[16,1024]{1,0:T(8,128)S(1)} %get-tuple-element.566), channel_id=4, replica_groups=mesh['seq'=8,'chan'=4] {'seq'}, dimensions={0}, use_global_device_ids=true | all-gather | bytes 589824 | tf_op jit(solution)/shard_map/all_gather | solution.py:25
  271.8 33.5 %all-gather.4 = f32[128,1024]{1,0:T(8,128)} all-gather(f32[16,1024]{1,0:T(8,128)} %get-tuple-element.570), channel_id=6, replica_groups=mesh['seq'=8,'chan'=4] {'seq'}, dimensions={0}, use_global_device_ids=true | all-gather | bytes 589824 | tf_op jit(solution)/shard_map/all_gather | solution.py:25
  305.3 33.3 %all-gather.1 = f32[128,1024]{1,0:T(8,128)} all-gather(f32[16,1024]{1,0:T(8,128)S(1)} %get-tuple-element.565), channel_id=3, replica_groups=mesh['seq'=8,'chan'=4] {'seq'}, dimensions={0}, use_global_device_ids=true | all-gather | bytes 589824 | tf_op jit(solution)/shard_map/all_gather | solution.py:25
  338.6 7.5 %while.91 = (s32[]{:T(128)}, f32[16,1024]{1,0:T(8,128)S(1)}, s32[]{:T(128)}, f32[8,16,1024]{2,1,0:T(8,128)}, f32[8,16,1024]{2,1,0:T(8,128)}, /*index=5*/s32[]{:T(128)}, s32[]{:T(128)}) while((s32[]{:T(128)}, f32[16,1024]{1,0:T(8,128)S(1)}, s32[]{:T(128)}, f32[8,16,1024]{2,1,0:T(8,128)}, f32[8,16,1024]{2,1,0:T(8,128)}, ...), condition=%wide.region_6.7_spmd.clone, body=%wide.region_5.6_spmd.clone.sunk | while | flops 65540 | bytes 262253 | solution.py:38
  346.1 33.2 %all-gather.3 = f32[128,1024]{1,0:T(8,128)} all-gather(f32[16,1024]{1,0:T(8,128)S(1)} %copy-done.3), channel_id=5, replica_groups=mesh['seq'=8,'chan'=4] {'seq'}, dimensions={0}, use_global_device_ids=true | all-gather | bytes 589824 | tf_op jit(solution)/shard_map/all_gather | solution.py:25
  379.3 7.5 %while.93 = (s32[]{:T(128)}, f32[16,1024]{1,0:T(8,128)S(1)}, s32[]{:T(128)}, f32[8,16,1024]{2,1,0:T(8,128)}, f32[8,16,1024]{2,1,0:T(8,128)}, /*index=5*/s32[]{:T(128)}, s32[]{:T(128)}, s32[]{:T(128)}, s32[]{:T(128)}) while((s32[]{:T(128)}, f32[16,1024]{1,0:T(8,128)S(1)}, s32[]{:T(128)}, f32[8,16,1024]{2,1,0:T(8,128)}, ...), condition=%wide.region_28.29_spmd.clone, body=%wide.region_27.28_spmd.clone.sunk | while | flops 65544 | bytes 262315 | solution.py:38
  386.9 43.7 %while.89 = (s32[]{:T(128)}, f32[16,1024]{1,0:T(8,128)S(1)}, f32[8,16,1024]{2,1,0:T(8,128)S(1)}, f32[8,16,1024]{2,1,0:T(8,128)}, f32[8,16,16]{2,1,0:T(8,128)}, /...) while((s32[]{:T(128)}, f32[16,1024]{1,0:T(8,128)S(1)}, ...), condition=%wide.region_46.47_spmd, body=%wide.region_29.46_spmd.sunk | while | flops 2408722 | bytes 2033121 | solution.py:67
  389.3 2.0 constant_dynamic-slice_fusion.229
  400.2 2.0 constant_dynamic-slice_fusion.229
  416.4 2.0 constant_dynamic-slice_fusion.229
  427.4 1.8 constant_dynamic-slice_fusion.229
  431.4 32.3 %while.88 = (s32[]{:T(128)}, f32[16,1024]{1,0:T(8,128)S(1)}, f32[8,16,1024]{2,1,0:T(8,128)S(1)}, f32[8,16,1024]{2,1,0:T(8,128)S(1)}, f32[8,16,16]{2,1,0:T(8,128)...) while((s32[]{:T(128)}, f32[16,1024]{1,0:T(8,128)S(1)}, ...), condition=%wide.region_24.25_spmd, body=%wide.region_7.24_spmd.sunk | while | flops 2490641 | bytes 2106965 | solution.py:67
  465.3 2.9 fusion.342
  468.2 25.5 %all-reduce.1 = bf16[128,2048]{1,0:T(8,128)(2,1)S(1)} all-reduce(f32[128,2048]{1,0:T(8,128)S(1)} %fusion.342), channel_id=1, replica_groups=mesh['seq'=8,'chan'=4] {'chan'}, use_global_device_ids=true, to_apply=%region_47.48 | all-reduce | flops 262144 | bytes 1572864 | tf_op jit(solution)/shard_map/psum | solution.py:159
  (853 shorter events, 139.4 us)
Async XLA Ops:
  6.5 153.8 %copy-start = (bf16[2,1024,160]{1,2,0:T(8,128)(2,1)S(1)}, bf16[2,1024,160]{1,2,0:T(8,128)(2,1)}, u32[]{:S(2)}) copy-start(bf16[2,1024,160]{1,2,0:T(8,128)(2,1)} %param.27) | copy-start | bytes 1966084
  6.5 130.2 %all-gather.8.cloned.1.call-start = ((), (), s32[]{:S(2)}) async-start(), calls=%async_computation | async-start | bytes 9437184 | tf_op jit(solution)/shard_map/all_gather | solution.py:101
  7.3 458.0 %all-gather.10.cloned.1.call-start = ((), (), s32[]{:S(2)}) async-start(), calls=%async_computation.1 | async-start | bytes 4718592 | tf_op jit(solution)/shard_map/all_gather | solution.py:156
  136.7 10.1 %copy-start.6 = (f32[2048]{0:T(1024)S(1)}, f32[2048]{0:T(1024)}, u32[]{:S(2)}) copy-start(f32[2048]{0:T(1024)} %param.23) | copy-start | bytes 24580
  152.0 7.5 %collective-permute-start.1 = (bf16[3,1024]{1,0:T(4,128)(2,1)S(1)}, bf16[3,1024]{1,0:T(4,128)(2,1)S(1)}, u32[]{:S(2)}, u32[]{:S(2)}) collective-permute-start(bf16[3,1024]{1,0:T(4,128)(2,1)S(1)} %bitcast.1151), channel_id=1, source_target_pairs={{4,0},{8,4},{12,8},{16,12},{20,16},{24,20},{28,24},{5,1},{9,5},{13... | collective-permute-start | bytes 18440 | tf_op jit(solution)/shard_map/ppermute | solution.py:18
  153.3 6.2 %collective-permute-start = (bf16[3,1024]{1,0:T(4,128)(2,1)S(1)}, bf16[3,1024]{1,0:T(4,128)(2,1)S(1)}, u32[]{:S(2)}, u32[]{:S(2)}) collective-permute-start(bf16[3,1024]{1,0:T(4,128)(2,1)S(1)} %bitcast.1150), channel_id=1, source_target_pairs={{0,4},{4,8},{8,12},{12,16},{16,20},{20,24},{24,28},{1,5},{5,9},{9,... | collective-permute-start | bytes 18440 | tf_op jit(solution)/shard_map/ppermute | solution.py:15
  174.5 53.3 %copy-start.1 = (f32[16,1024]{1,0:T(8,128)S(1)}, f32[16,1024]{1,0:T(8,128)}, u32[]{:S(2)}) copy-start(f32[16,1024]{1,0:T(8,128)} %custom-call.1) | copy-start | bytes 196612
  174.5 53.3 %copy-start.2 = (f32[16,1024]{1,0:T(8,128)S(1)}, f32[16,1024]{1,0:T(8,128)}, u32[]{:S(2)}) copy-start(f32[16,1024]{1,0:T(8,128)} %custom-call) | copy-start | bytes 196612
  227.7 118.4 %copy-start.3 = (f32[16,1024]{1,0:T(8,128)S(1)}, f32[16,1024]{1,0:T(8,128)}, u32[]{:S(2)}) copy-start(f32[16,1024]{1,0:T(8,128)} %get-tuple-element.569) | copy-start | bytes 196612
  237.3 149.5 %copy-start.5 = (f32[8,16,16]{2,1,0:T(8,128)}, f32[8,16,16]{2,1,0:T(8,128)S(1)}, u32[]{:S(2)}) copy-start(f32[8,16,16]{2,1,0:T(8,128)S(1)} %get-tuple-element.2560) | copy-start | bytes 24580
  430.6 0.8 copy-start.4
Sparse Core Ops, SparseCore 0:
  9.5 127.1 all-gather.7
  138.7 72.8 all-gather.9
